TPU v7x, 32 devices: a whole 2x2x4 slice. The times are simulated.
32 devices in a mesh: gx: 8 (over z, x), col: 4 (over y, core).
Axes of the slice: x: 2, y: 2, z: 4, core: 2. Of those that a mesh axis runs over, the one named last changes fastest.
Arguments:
- grid_field: bfloat16 [64, 32, 256, 128], P('col', 'gx'), may hold values from -6 to 6
- tucker_core: float32 [2, 32, 32, 8, 8, 4], P(None, 'col'), may hold values from -0.5 to 0.5
- in_factor: float32 [64, 32], P('col'), may hold values from -0.75 to 0.75
- out_factor: float32 [64, 32], P('col'), may hold values from -1 to 1
- x_factor: float32 [32, 8], replicated, may hold values from -4 to 4
- y_factor: float32 [32, 8], replicated, may hold values from -4 to 4
- z_factor: float32 [16, 4], replicated, may hold values from -4 to 4
- kx_reach: int32 [32, 16], replicated, may hold values from 1 to 17
Outputs:
- spectral_out: bfloat16 [64, 32, 256, 128], P('col', 'gx')
All inputs are finite; a program needn't handle non-finite values.
Results may differ from a plain program's by a relative error of at most 0.001.
Values sent between devices are 32-bit elements; how exact they have to be, the bound alone decides.
A program may use at most 64 MiB of HBM per device.

v0:
```python
import math
import jax
import jax.numpy as jnp
from jax import lax
from jax.sharding import PartitionSpec as P


def slot_freq(slot_count):
    slot_index = jnp.arange(slot_count, dtype=jnp.int32)
    return jnp.where(slot_index < slot_count // 2, slot_index, slot_index - slot_count)


def phase_table(positions, extent, slot_count, direction):
    phase_steps = positions[:, None] * slot_freq(slot_count)[None, :] % extent
    radians = 2.0 * math.pi / extent * phase_steps.astype(jnp.float32)
    norm_scale = 1.0 / math.sqrt(extent)
    cosine = jnp.cos(radians) * norm_scale
    sine_part = direction * jnp.sin(radians) * norm_scale
    return jnp.stack([jnp.stack([cosine, -sine_part], 1), jnp.stack([sine_part, cosine], 1)], 1)


def z_tables(grid_z, modes_z):
    z_index = jnp.arange(grid_z, dtype=jnp.int32)
    kz_index = jnp.arange(modes_z, dtype=jnp.int32)
    phase_steps = z_index[:, None] * kz_index[None, :] % grid_z
    radians = 2.0 * math.pi / grid_z * phase_steps.astype(jnp.float32)
    norm_scale = 1.0 / math.sqrt(grid_z)
    cosine = jnp.cos(radians) * norm_scale
    sine_part = jnp.sin(radians) * norm_scale
    forward = jnp.stack([cosine, -sine_part], 1)
    weight = jnp.where(kz_index == 0, 1.0, 2.0).astype(jnp.float32)
    backward = jnp.stack([(cosine * weight[None, :]).T, -(sine_part * weight[None, :]).T], 0)
    return (forward, backward)


def per_device(
    grid_field, tucker_core, in_factor, out_factor, x_factor, y_factor, z_factor, kx_reach
):
    highest = lax.Precision.HIGHEST
    channels, planes, grid_y, grid_z = grid_field.shape
    modes_x = x_factor.shape[0]
    modes_y = y_factor.shape[0]
    modes_z = z_factor.shape[0]
    width_gx = lax.axis_size("gx")
    grid_x = planes * width_gx
    columns = modes_y * modes_z
    col_dev = columns // width_gx
    slab_index = lax.axis_index("gx")
    z_forward, z_backward = z_tables(grid_z, modes_z)
    y_forward = phase_table(jnp.arange(grid_y, dtype=jnp.int32), grid_y, modes_y, 1.0)
    x_forward = phase_table(jnp.arange(grid_x, dtype=jnp.int32), grid_x, modes_x, 1.0)
    values = grid_field.astype(jnp.float32)
    z_spectrum = jnp.einsum("cxyz,zpl->cxply", values, z_forward, precision=highest)
    y_spectrum = jnp.einsum("cxply,ypqj->qcxjl", z_spectrum, y_forward, precision=highest)
    y_spectrum = y_spectrum.reshape(2, channels, planes, columns)
    first_col = slab_index * col_dev
    reach_dev = lax.dynamic_slice_in_dim(kx_reach.reshape(-1), first_col, col_dev)
    kept_mask = (jnp.abs(slot_freq(modes_x))[:, None] < reach_dev[None, :]).astype(jnp.float32)
    arrived = lax.all_to_all(y_spectrum, "gx", split_axis=3, concat_axis=2, tiled=True)
    spectrum = jnp.einsum("pcxm,xpqk->qckm", arrived, x_forward, precision=highest)
    partial_value = jnp.einsum("qckm,cr->qrkm", spectrum, in_factor, precision=highest)
    amplitude = lax.psum_scatter(partial_value, "col", scatter_dimension=1, tiled=True)
    amplitude = amplitude * kept_mask[None, None]
    column = first_col + jnp.arange(col_dev, dtype=jnp.int32)
    pick_y = (column[:, None] // modes_z == jnp.arange(modes_y, dtype=jnp.int32)[None, :]).astype(
        jnp.float32
    )
    pick_z = (column[:, None] % modes_z == jnp.arange(modes_z, dtype=jnp.int32)[None, :]).astype(
        jnp.float32
    )
    y_rows = jnp.dot(pick_y, y_factor, precision=highest)
    z_rows = jnp.dot(pick_z, z_factor, precision=highest)
    core_cols = jnp.einsum("prsabe,mb,me->prsam", tucker_core, y_rows, z_rows, precision=highest)
    kernel = jnp.einsum("prsam,ka->prskm", core_cols, x_factor, precision=highest)
    mixed_re = jnp.einsum("rskm,rkm->skm", kernel[0], amplitude[0], precision=highest) - jnp.einsum(
        "rskm,rkm->skm", kernel[1], amplitude[1], precision=highest
    )
    mixed_im = jnp.einsum("rskm,rkm->skm", kernel[0], amplitude[1], precision=highest) + jnp.einsum(
        "rskm,rkm->skm", kernel[1], amplitude[0], precision=highest
    )
    mixed_sum = lax.psum(jnp.stack([mixed_re, mixed_im]), "col")
    out_spec = jnp.einsum("os,qskm->qokm", out_factor, mixed_sum, precision=highest)
    x_backward = phase_table(jnp.arange(grid_x, dtype=jnp.int32), grid_x, modes_x, -1.0)
    x_values = jnp.einsum("pckm,xpqk->qcxm", out_spec, x_backward, precision=highest)
    returned = lax.all_to_all(x_values, "gx", split_axis=2, concat_axis=3, tiled=True)
    returned = returned.reshape(2, channels, planes, modes_y, modes_z)
    y_backward = phase_table(jnp.arange(grid_y, dtype=jnp.int32), grid_y, modes_y, -1.0)
    y_values = jnp.einsum("pcxjl,ypqj->cxqly", returned, y_backward, precision=highest)
    result = jnp.einsum("cxqly,qlz->cxyz", y_values, z_backward, precision=highest)
    return result.astype(jnp.bfloat16)


def solution(mesh):
    return jax.shard_map(
        per_device,
        mesh=mesh,
        in_specs=(
            P("col", "gx", None, None),
            P(None, "col", None, None, None, None),
            P("col", None),
            P("col", None),
            P(),
            P(),
            P(),
            P(),
        ),
        out_specs=P("col", "gx", None, None),
        check_vma=False,
    )
```

profile of v0, /device:TPU:0, one launch (start us, length us, event | category | flops | bytes accessed | tf_op | source)
XLA Modules:
  0.0 163.9 jit_solution(2289638814313260271)
XLA Ops:
  6.5 0.1 multiply_negate_fusion.1
  6.6 0.2 fusion.58
  6.8 6.5 %fusion = f32[2,16,16,4,256]{4,1,0,3,2:T(8,128)S(1)} fusion(bf16[16,4,256,128]{3,2,1,0:T(8,128)(2,1)} %param.8, f32[128,1,16]{0,2,1:T(8,128)S(1)} %get-tuple-element.35, f32[128,1,16]{0,2,1:T(8,128)S(1)} %get-tuple-element.36), kind=kOutput, calls=%fused_computation.3 | convolution fusion | flops 805310464 | bytes 6307840 | tf_op jit(solution)/shard_map/cxyz,zpl->cxply/dot_general | solution.py:53
  13.4 1.8 %fusion.9 = f32[2,16,4,32,16]{3,4,2,1,0:T(8,128)S(1)} fusion(f32[2,16,16,4,256]{4,1,0,3,2:T(8,128)S(1)} %fusion, f32[256,1,2,32]{0,3,1,2:T(8,128)S(1)} %get-tuple-element.14, f32[256,1,2,32]{0,3,1,2:T(8,128)S(1)} %get-tuple-element.15), kind=kOutput, calls=%fused_computation.19 | convolution fusion | flops 402685952 | bytes 2490368 | tf_op jit(solution)/shard_map/cxply,ypqj->qcxjl/dot_general | solution.py:54
  15.2 2.7 %copy.101 = f32[2,16,4,32,16]{1,2,0,4,3:T(4,128)} copy(f32[2,16,4,32,16]{3,4,2,1,0:T(8,128)S(1)} %fusion.9) | data formatting | bytes 524288 | tf_op jit(solution)/shard_map/reshape | solution.py:55
  17.9 3.8 %reshape.675 = f32[8,1,8192]{2,1,0:T(1,128)} reshape(f32[512,2,4,16]{3,2,1,0:T(4,128)} %bitcast.192) | data formatting | bytes 524288
  21.6 7.3 %all-to-all-start = ((f32[8,1,8192]{2,1,0:T(1,128)}), f32[8,1,8192]{2,1,0:T(1,128)S(1)}, u32[]{:S(2)}, u32[]{:S(2)}) async-start(f32[8,1,8192]{2,1,0:T(1,128)} %reshape.675), calls=%async_computation | async-start | bytes 524288 | tf_op jit(solution)/shard_map/all_to_all | solution.py:59
  28.9 0.0 reduce-scatter.2.cloned.1.call-start
  29.0 0.2 fusion.77
  29.2 0.2 fusion.40
  29.4 8.5 %all-to-all-done = f32[8,1,8192]{2,1,0:T(1,128)S(1)} async-done(((f32[8,1,8192]{2,1,0:T(1,128)}), f32[8,1,8192]{2,1,0:T(1,128)S(1)}, u32[]{:S(2)}, u32[]{:S(2)}) %all-to-all-start) | async-done | bytes 262176 | tf_op jit(solution)/shard_map/all_to_all | solution.py:59
  37.8 0.5 broadcast.967
  38.3 1.2 reduce.8
  39.5 2.8 %reshape.676 = f32[512,2,4,16]{3,2,1,0:T(4,128)} reshape(f32[8,8192]{1,0:T(8,128)S(1)} %reduce.8) | data formatting | bytes 524288
  42.3 1.9 %copy.103 = f32[2,16,4,8,64]{4,1,2,3,0:T(8,128)S(1)} copy(f32[2,16,4,8,64]{1,2,0,4,3:T(4,128)} %bitcast.191) | data formatting | bytes 524288 | tf_op jit(solution)/shard_map/all_to_all | solution.py:59
  44.2 0.7 convolution_bitcast_fusion.4
  44.9 2.2 %convolution_bitcast_fusion.2 = f32[2,32,32,64]{3,1,2,0:T(8,128)} fusion(f32[2,16,32,64]{3,2,1,0:T(8,128)S(1)} %convolution_bitcast_fusion.4, f32[16,32]{1,0:T(8,128)S(1)} %copy-done.1), kind=kOutput, calls=%fused_computation.18 | convolution fusion | flops 25165824 | bytes 788480 | tf_op jit(solution)/shard_map/qckm,cr->qrkm/dot_general | solution.py:61
  47.1 0.0 reduce-scatter.2.cloned.1.call-update
  47.2 0.2 all-reduce.2.cloned.1.call-start
  47.4 0.2 fusion.41
  47.6 0.1 copy.39
  47.7 0.1 reshape.644
  47.8 0.1 dynamic_slice.3
  47.9 0.0 copy-start.4
  47.9 3.7 %convolution_bitcast_fusion.1 = f32[2,8,32,8,64]{4,2,3,1,0:T(8,128)S(1)} fusion(f32[2,8,32,8,8,4]{2,5,4,3,1,0:T(4,128)S(1)} %copy-done, f32[64,8]{0,1:T(8,128)S(1)} %fusion.40, f32[64,4]{0,1:T(4,128)S(1)} %fusion.41), kind=kOutput, calls=%fused_computation.17 | convolution fusion | flops 100665344 | bytes 1575936 | tf_op jit(solution)/shard_map/prsabe,mb,me->prsam/dot_general | solution.py:73
  51.6 0.1 compare_convert_fusion
  51.7 9.0 %convolution_bitcast_fusion = f32[2,8,32,32,64]{4,3,2,1,0:T(8,128)} fusion(f32[2,8,32,8,64]{4,2,3,1,0:T(8,128)S(1)} %convolution_bitcast_fusion.1, f32[32,8]{0,1:T(8,128)S(1)} %copy-done.4), kind=kOutput, calls=%fused_computation.9 | convolution fusion | flops 100663296 | bytes 5243904 | tf_op jit(solution)/shard_map/prsam,ka->prskm/dot_general | solution.py:74
  60.7 10.5 %reduce-scatter.2.cloned.1.call-done = f32[2,8,32,64]{3,1,2,0:T(8,128)} async-done(((f32[2,32,32,64]{3,1,2,0:T(8,128)}), f32[2,8,32,64]{3,1,2,0:T(8,128)}) %reduce-scatter.2.cloned.1.call-update) | async-done | bytes 131088 | tf_op jit(solution)/shard_map/reduce_scatter | solution.py:62
  71.2 1.0 broadcast_multiply_fusion
  72.3 4.6 %multiply_reduce_fusion.3 = (f32[32,64,32]{1,0,2:T(8,128)S(1)}, f32[32,64,32]{1,0,2:T(8,128)S(1)}, f32[32,64,32]{1,0,2:T(8,128)S(1)}, f32[32,64,32]{1,0,2:T(8,128)S(1)}) fusion(f32[2,8,32,32,64]{4,3,2,1,0:T(8,128)} %convolution_bitcast_fusion, f32[32,64,8]{1,0,2:T(8,128)S(1)} %copy.107, f32[32,64,8]{1,0,2:T(8,128)S(1)} %copy.108), kind=kLoop, calls=%fused_computation.8 | loop fusion | flops 3932160 | bytes 5373952
  76.9 0.6 fusion.15
  77.5 0.6 fusion.14
  78.1 1.1 pad_maximum_fusion
  79.2 0.0 all-reduce.2.cloned.1.call-update
  79.2 36.5 %all-reduce.2.cloned.1.call-done = f32[2,32,32,64]{3,1,2,0:T(8,128)} async-done(((f32[2,32,32,64]{3,1,2,0:T(8,128)}), f32[2,32,32,64]{3,1,2,0:T(8,128)}) %all-reduce.2.cloned.1.call-update) | async-done | bytes 524304 | tf_op jit(solution)/shard_map/psum | solution.py:81
  115.7 1.9 %convolution_bitcast_fusion.5 = f32[2,16,32,64]{3,1,2,0:T(8,128)S(1)} fusion(f32[2,32,32,64]{3,1,2,0:T(8,128)} %all-reduce.2.cloned.1.call-done, f32[16,32]{1,0:T(8,128)S(1)} %copy-done.2), kind=kOutput, calls=%fused_computation.22 | convolution fusion | flops 25165824 | bytes 788480 | tf_op jit(solution)/shard_map/os,qskm->qokm/dot_general | solution.py:82
  117.6 0.7 convolution_bitcast_fusion.3
  118.3 0.3 copy.140
  118.6 1.0 reshape.677
  119.6 5.5 %all-to-all-start.1 = ((f32[8,1,8192]{2,1,0:T(1,128)}), f32[8,1,8192]{2,1,0:T(1,128)S(1)}, u32[]{:S(2)}, u32[]{:S(2)}) async-start(f32[8,1,8192]{2,1,0:T(1,128)} %reshape.677), calls=%async_computation.2 | async-start | bytes 524288 | tf_op jit(solution)/shard_map/all_to_all | solution.py:85
  125.2 0.1 cosine_multiply_fusion.2
  125.2 8.4 %all-to-all-done.1 = f32[8,1,8192]{2,1,0:T(1,128)S(1)} async-done(((f32[8,1,8192]{2,1,0:T(1,128)}), f32[8,1,8192]{2,1,0:T(1,128)S(1)}, u32[]{:S(2)}, u32[]{:S(2)}) %all-to-all-start.1) | async-done | bytes 262176 | tf_op jit(solution)/shard_map/all_to_all | solution.py:85
  133.6 1.2 reduce.9
  134.8 0.2 reshape.678
  135.0 0.3 copy.139
  135.3 1.8 %reshape.645 = f32[2,16,4,32,16]{4,3,2,1,0:T(8,128)} reshape(f32[2,16,4,8,64]{4,3,2,1,0:T(8,128)S(1)} %bitcast.194) | data formatting | bytes 524288 | tf_op jit(solution)/shard_map/reshape | solution.py:86
  137.1 5.1 %fusion.3 = f32[256,2,16,4,16,1]{0,4,1,5,3,2:T(8,128)S(1)} fusion(f32[256,1,2,32]{0,3,2,1:T(8,128)S(1)} %get-tuple-element.16, f32[256,1,2,32]{0,3,2,1:T(8,128)S(1)} %get-tuple-element.13, f32[2,16,4,32,16]{4,3,2,1,0:T(8,128)} %reshape.645), kind=kOutput, calls=%fused_computation.11 | convolution fusion | flops 402685952 | bytes 2490368 | tf_op jit(solution)/shard_map/pcxjl,ypqj->cxqly/dot_general | solution.py:88
  142.2 14.9 %bitcast_convert_fusion = bf16[16,4,256,128]{3,2,1,0:T(8,128)(2,1)} fusion(f32[256,2,16,4,16,1]{0,4,1,5,3,2:T(8,128)S(1)} %fusion.3, f32[1,16,128]{2,1,0:T(8,128)S(1)} %get-tuple-element.22, f32[1,16,128]{2,1,0:T(8,128)S(1)} %get-tuple-element.21), kind=kOutput, calls=%fused_computation | convolution fusion | flops 807407616 | bytes 6307840 | tf_op jit(solution)/shard_map/cxqly,qlz->cxyz/dot_general | solution.py:89
  (22 shorter events, 0.2 us)
Async XLA Ops:
  6.5 41.3 %copy-start = (f32[2,8,32,8,8,4]{2,5,4,3,1,0:T(4,128)S(1)}, f32[2,8,32,8,8,4]{2,5,4,3,1,0:T(4,128)}, u32[]{:S(2)}) copy-start(f32[2,8,32,8,8,4]{2,5,4,3,1,0:T(4,128)} %param.9) | copy-start | bytes 1572868
  17.9 11.3 %copy-start.5 = (f32[32,8]{0,1:T(8,128)S(1)}, f32[32,8]{0,1:T(8,128)}, u32[]{:S(2)}) copy-start(f32[32,8]{0,1:T(8,128)} %param.13) | copy-start | bytes 3076
  21.6 16.2 %all-to-all-start = ((f32[8,1,8192]{2,1,0:T(1,128)}), f32[8,1,8192]{2,1,0:T(1,128)S(1)}, u32[]{:S(2)}, u32[]{:S(2)}) async-start(f32[8,1,8192]{2,1,0:T(1,128)} %reshape.675), calls=%async_computation | async-start | bytes 524288 | tf_op jit(solution)/shard_map/all_to_all | solution.py:59
  28.9 42.3 %reduce-scatter.2.cloned.1.call-start = ((), (), s32[]{:S(2)}) async-start(), calls=%async_computation.3 | async-start | bytes 1310720 | tf_op jit(solution)/shard_map/reduce_scatter | solution.py:62
  42.3 2.6 %copy-start.1 = (f32[16,32]{1,0:T(8,128)S(1)}, f32[16,32]{1,0:T(8,128)}, u32[]{:S(2)}) copy-start(f32[16,32]{1,0:T(8,128)} %param.10) | copy-start | bytes 6148
  44.2 3.2 %copy-start.6 = (f32[16,4]{0,1:T(4,128)S(1)}, f32[16,4]{0,1:T(4,128)}, u32[]{:S(2)}) copy-start(f32[16,4]{0,1:T(4,128)} %param.14) | copy-start | bytes 772
  44.2 3.4 %copy-start.3 = (s32[32,16]{0,1:T(8,128)S(1)}, s32[32,16]{0,1:T(8,128)}, u32[]{:S(2)}) copy-start(s32[32,16]{0,1:T(8,128)} %param.15) | copy-start | bytes 6148
  47.2 68.5 %all-reduce.2.cloned.1.call-start = ((), (), s32[]{:S(2)}) async-start(), calls=%async_computation.4 | async-start | bytes 2097152 | tf_op jit(solution)/shard_map/psum | solution.py:81
  47.9 3.8 %copy-start.4 = (f32[32,8]{0,1:T(8,128)S(1)}, f32[32,8]{0,1:T(8,128)}, u32[]{:S(2)}) copy-start(f32[32,8]{0,1:T(8,128)} %param.12) | copy-start | bytes 3076
  77.5 38.2 %copy-start.2 = (f32[16,32]{1,0:T(8,128)S(1)}, f32[16,32]{1,0:T(8,128)}, u32[]{:S(2)}) copy-start(f32[16,32]{1,0:T(8,128)} %param.11) | copy-start | bytes 6148
  119.6 14.0 %all-to-all-start.1 = ((f32[8,1,8192]{2,1,0:T(1,128)}), f32[8,1,8192]{2,1,0:T(1,128)S(1)}, u32[]{:S(2)}, u32[]{:S(2)}) async-start(f32[8,1,8192]{2,1,0:T(1,128)} %reshape.677), calls=%async_computation.2 | async-start | bytes 524288 | tf_op jit(solution)/shard_map/all_to_all | solution.py:85
Sparse Core Ops, SparseCore 0:
  47.3 23.8 reduce-scatter.1
  79.3 36.2 all-reduce.1
where the time goes:
time: 164 us
  waiting for transfers between devices  63.9 us (39%)
  matrix products  46.9 us (29%)
  local copies, waits for them, and re-layouts  15.6 us (10%)
  between operations  13.6 us (8%)
  starting transfers between devices  13.1 us (8%)
  other arithmetic  10.8 us (7%)
    psum x1, waiting for transfers between devices, per_device(): mixed_sum = lax.psum(jnp.stack([mixed_re, mixed_im]), 'col')  36.5 us
    dot_general x1, matrix products, per_device(): jnp.einsum('cxqly,qlz->cxyz', y_values, z_backward, precision=highest)  14.9 us
    reduce_scatter x1, waiting for transfers between devices, per_device(): lax.psum_scatter(partial_value, 'col', scatter_dimension=1, tiled=True)  10.5 us
    dot_general x1, matrix products, per_device(): jnp.einsum('prsam,ka->prskm', core_cols, x_factor, precision=highest)  9.02 us
    all_to_all x1, waiting for transfers between devices, per_device(): lax.all_to_all(y_spectrum, 'gx', split_axis=3, concat_axis=2, tiled=True)  8.47 us
    all_to_all x1, waiting for transfers between devices, per_device(): lax.all_to_all(x_values, 'gx', split_axis=2, concat_axis=3, tiled=True)  8.4 us
    unnamed x22, local copies, waits for them, and re-layouts  7.99 us
    all_to_all x1, starting transfers between devices, per_device(): lax.all_to_all(y_spectrum, 'gx', split_axis=3, concat_axis=2, tiled=True)  7.29 us
  transfers between devices with their start and end apart: 4, of which 4 were waited for; matrix products, arithmetic and copies ran while one was open for 8% of the time, Pallas kernels for 0%

commit v1 on v0

--- a/solution.py
+++ b/solution.py
@@ -82,7 +82,10 @@
     out_spec = jnp.einsum("os,qskm->qokm", out_factor, mixed_sum, precision=highest)
     x_backward = phase_table(jnp.arange(grid_x, dtype=jnp.int32), grid_x, modes_x, -1.0)
     x_values = jnp.einsum("pckm,xpqk->qcxm", out_spec, x_backward, precision=highest)
-    returned = lax.all_to_all(x_values, "gx", split_axis=2, concat_axis=3, tiled=True)
+    returned = jnp.concatenate(
+        lax.all_to_all(jnp.stack(jnp.split(x_values, lax.axis_size("gx"), axis=2)), "gx", 0, 0),
+        axis=3,
+    )
     returned = returned.reshape(2, channels, planes, modes_y, modes_z)
     y_backward = phase_table(jnp.arange(grid_y, dtype=jnp.int32), grid_y, modes_y, -1.0)
     y_values = jnp.einsum("pcxjl,ypqj->cxqly", returned, y_backward, precision=highest)

time: 164 us -> 165 us (level)
    another operation x0 -> x2, local copies, waits for them, and re-layouts: none -> 1.82 us  [the longest x1 1.79 us: per_device(): returned = returned.reshape(2, channels, planes, modes_y, modes_z)]
    unnamed x22 -> x29, local copies, waits for them, and re-layouts: 7.99 us -> 8.5 us
where the time goes in v1:
time: 165 us; the launch traced here: 164 us
  waiting for transfers between devices  63.9 us (39%)
  matrix products  46.9 us (28%)
  local copies, waits for them, and re-layouts  15.8 us (10%)
  between operations  13.6 us (8%)
  starting transfers between devices  13.1 us (8%)
  other arithmetic  10.8 us (7%)
    psum x1, waiting for transfers between devices, per_device(): mixed_sum = lax.psum(jnp.stack([mixed_re, mixed_im]), 'col')  36.5 us
    dot_general x1, matrix products, per_device(): jnp.einsum('cxqly,qlz->cxyz', y_values, z_backward, precision=highest)  14.9 us
    reduce_scatter x1, waiting for transfers between devices, per_device(): lax.psum_scatter(partial_value, 'col', scatter_dimension=1, tiled=True)  10.5 us
    dot_general x1, matrix products, per_device(): jnp.einsum('prsam,ka->prskm', core_cols, x_factor, precision=highest)  9.02 us
    unnamed x29, local copies, waits for them, and re-layouts  8.5 us
    all_to_all x1, waiting for transfers between devices, per_device(): lax.all_to_all(y_spectrum, 'gx', split_axis=3, concat_axis=2, tiled=True)  8.47 us
    all_to_all x1, waiting for transfers between devices, per_device(): lax.all_to_all(jnp.stack(jnp.split(x_values, lax.axis_size('gx'), axis=2)...  8.4 us
    all_to_all x1, starting transfers between devices, per_device(): lax.all_to_all(y_spectrum, 'gx', split_axis=3, concat_axis=2, tiled=True)  7.29 us
  transfers between devices with their start and end apart: 4, of which 4 were waited for; matrix products, arithmetic and copies ran while one was open for 8% of the time, Pallas kernels for 0%

profile of v1, /device:TPU:0, one launch (start us, length us, event | category | flops | bytes accessed | tf_op | source)
XLA Modules:
  0.0 164.1 jit_solution(13735980997955982344)
XLA Ops:
  6.5 0.1 multiply_negate_fusion.1
  6.6 0.2 fusion.66
  6.8 6.5 %fusion = f32[2,16,16,4,256]{4,1,0,3,2:T(8,128)S(1)} fusion(bf16[16,4,256,128]{3,2,1,0:T(8,128)(2,1)} %param.8, f32[128,1,16]{0,2,1:T(8,128)S(1)} %get-tuple-element.35, f32[128,1,16]{0,2,1:T(8,128)S(1)} %get-tuple-element.36), kind=kOutput, calls=%fused_computation.3 | convolution fusion | flops 805310464 | bytes 6307840 | tf_op jit(solution)/shard_map/cxyz,zpl->cxply/dot_general | solution.py:53
  13.4 1.8 %fusion.9 = f32[2,16,4,32,16]{3,4,2,1,0:T(8,128)S(1)} fusion(f32[2,16,16,4,256]{4,1,0,3,2:T(8,128)S(1)} %fusion, f32[256,1,2,32]{0,3,1,2:T(8,128)S(1)} %get-tuple-element.14, f32[256,1,2,32]{0,3,1,2:T(8,128)S(1)} %get-tuple-element.15), kind=kOutput, calls=%fused_computation.19 | convolution fusion | flops 402685952 | bytes 2490368 | tf_op jit(solution)/shard_map/cxply,ypqj->qcxjl/dot_general | solution.py:54
  15.2 2.7 %copy.99 = f32[2,16,4,32,16]{1,2,0,4,3:T(4,128)} copy(f32[2,16,4,32,16]{3,4,2,1,0:T(8,128)S(1)} %fusion.9) | data formatting | bytes 524288 | tf_op jit(solution)/shard_map/reshape | solution.py:55
  17.9 3.8 %reshape.674 = f32[8,1,8192]{2,1,0:T(1,128)} reshape(f32[512,2,4,16]{3,2,1,0:T(4,128)} %bitcast.217) | data formatting | bytes 524288
  21.6 7.3 %all-to-all-start = ((f32[8,1,8192]{2,1,0:T(1,128)}), f32[8,1,8192]{2,1,0:T(1,128)S(1)}, u32[]{:S(2)}, u32[]{:S(2)}) async-start(f32[8,1,8192]{2,1,0:T(1,128)} %reshape.674), calls=%async_computation | async-start | bytes 524288 | tf_op jit(solution)/shard_map/all_to_all | solution.py:59
  28.9 0.0 reduce-scatter.2.cloned.1.call-start
  29.0 0.2 fusion.85
  29.2 0.2 fusion.48
  29.4 8.5 %all-to-all-done = f32[8,1,8192]{2,1,0:T(1,128)S(1)} async-done(((f32[8,1,8192]{2,1,0:T(1,128)}), f32[8,1,8192]{2,1,0:T(1,128)S(1)}, u32[]{:S(2)}, u32[]{:S(2)}) %all-to-all-start) | async-done | bytes 262176 | tf_op jit(solution)/shard_map/all_to_all | solution.py:59
  37.8 0.5 broadcast.967
  38.3 1.2 reduce.8
  39.5 2.8 %reshape.675 = f32[512,2,4,16]{3,2,1,0:T(4,128)} reshape(f32[8,8192]{1,0:T(8,128)S(1)} %reduce.8) | data formatting | bytes 524288
  42.3 1.9 %copy.101 = f32[2,16,4,8,64]{4,1,2,3,0:T(8,128)S(1)} copy(f32[2,16,4,8,64]{1,2,0,4,3:T(4,128)} %bitcast.216) | data formatting | bytes 524288 | tf_op jit(solution)/shard_map/all_to_all | solution.py:59
  44.2 0.0 copy-start.6
  44.2 0.7 convolution_bitcast_fusion.4
  44.9 2.2 %convolution_bitcast_fusion.2 = f32[2,32,32,64]{3,1,2,0:T(8,128)} fusion(f32[2,16,32,64]{3,2,1,0:T(8,128)S(1)} %convolution_bitcast_fusion.4, f32[16,32]{1,0:T(8,128)S(1)} %copy-done.1), kind=kOutput, calls=%fused_computation.18 | convolution fusion | flops 25165824 | bytes 788480 | tf_op jit(solution)/shard_map/qckm,cr->qrkm/dot_general | solution.py:61
  47.1 0.0 reduce-scatter.2.cloned.1.call-update
  47.2 0.2 all-reduce.2.cloned.1.call-start
  47.4 0.2 fusion.49
  47.6 0.1 copy.38
  47.7 0.1 reshape.643
  47.8 0.1 dynamic_slice.3
  47.9 0.0 copy-start.4
  47.9 3.7 %convolution_bitcast_fusion.1 = f32[2,8,32,8,64]{4,2,3,1,0:T(8,128)S(1)} fusion(f32[2,8,32,8,8,4]{2,5,4,3,1,0:T(4,128)S(1)} %copy-done, f32[64,8]{0,1:T(8,128)S(1)} %fusion.48, f32[64,4]{0,1:T(4,128)S(1)} %fusion.49), kind=kOutput, calls=%fused_computation.17 | convolution fusion | flops 100665344 | bytes 1575936 | tf_op jit(solution)/shard_map/prsabe,mb,me->prsam/dot_general | solution.py:73
  51.6 0.1 compare_convert_fusion
  51.7 9.0 %convolution_bitcast_fusion = f32[2,8,32,32,64]{4,3,2,1,0:T(8,128)} fusion(f32[2,8,32,8,64]{4,2,3,1,0:T(8,128)S(1)} %convolution_bitcast_fusion.1, f32[32,8]{0,1:T(8,128)S(1)} %copy-done.4), kind=kOutput, calls=%fused_computation.9 | convolution fusion | flops 100663296 | bytes 5243904 | tf_op jit(solution)/shard_map/prsam,ka->prskm/dot_general | solution.py:74
  60.7 10.5 %reduce-scatter.2.cloned.1.call-done = f32[2,8,32,64]{3,1,2,0:T(8,128)} async-done(((f32[2,32,32,64]{3,1,2,0:T(8,128)}), f32[2,8,32,64]{3,1,2,0:T(8,128)}) %reduce-scatter.2.cloned.1.call-update) | async-done | bytes 131088 | tf_op jit(solution)/shard_map/reduce_scatter | solution.py:62
  71.2 1.0 broadcast_multiply_fusion
  72.3 4.6 %multiply_reduce_fusion.3 = (f32[32,64,32]{1,0,2:T(8,128)S(1)}, f32[32,64,32]{1,0,2:T(8,128)S(1)}, f32[32,64,32]{1,0,2:T(8,128)S(1)}, f32[32,64,32]{1,0,2:T(8,128)S(1)}) fusion(f32[2,8,32,32,64]{4,3,2,1,0:T(8,128)} %convolution_bitcast_fusion, f32[32,64,8]{1,0,2:T(8,128)S(1)} %copy.105, f32[32,64,8]{1,0,2:T(8,128)S(1)} %copy.106), kind=kLoop, calls=%fused_computation.8 | loop fusion | flops 3932160 | bytes 5373952
  76.9 0.6 fusion.15
  77.5 0.6 fusion.14
  78.1 1.1 pad_maximum_fusion
  79.2 0.0 all-reduce.2.cloned.1.call-update
  79.2 36.5 %all-reduce.2.cloned.1.call-done = f32[2,32,32,64]{3,1,2,0:T(8,128)} async-done(((f32[2,32,32,64]{3,1,2,0:T(8,128)}), f32[2,32,32,64]{3,1,2,0:T(8,128)}) %all-reduce.2.cloned.1.call-update) | async-done | bytes 524304 | tf_op jit(solution)/shard_map/psum | solution.py:81
  115.7 1.9 %convolution_bitcast_fusion.5 = f32[2,16,32,64]{3,1,2,0:T(8,128)S(1)} fusion(f32[2,32,32,64]{3,1,2,0:T(8,128)} %all-reduce.2.cloned.1.call-done, f32[16,32]{1,0:T(8,128)S(1)} %copy-done.2), kind=kOutput, calls=%fused_computation.22 | convolution fusion | flops 25165824 | bytes 788480 | tf_op jit(solution)/shard_map/os,qskm->qokm/dot_general | solution.py:82
  117.6 0.7 convolution_bitcast_fusion.3
  118.5 1.2 reshape.676
  119.7 5.5 %all-to-all-start.1 = ((f32[8,1,8192]{2,1,0:T(1,128)}), f32[8,1,8192]{2,1,0:T(1,128)S(1)}, u32[]{:S(2)}, u32[]{:S(2)}) async-start(f32[8,1,8192]{2,1,0:T(1,128)} %reshape.676), calls=%async_computation.2 | async-start | bytes 524288 | tf_op jit(solution)/shard_map/all_to_all | solution.py:86
  125.3 0.1 cosine_multiply_fusion.2
  125.3 8.4 %all-to-all-done.1 = f32[8,1,8192]{2,1,0:T(1,128)S(1)} async-done(((f32[8,1,8192]{2,1,0:T(1,128)}), f32[8,1,8192]{2,1,0:T(1,128)S(1)}, u32[]{:S(2)}, u32[]{:S(2)}) %all-to-all-start.1) | async-done | bytes 262176 | tf_op jit(solution)/shard_map/all_to_all | solution.py:86
  133.7 1.2 reduce.9
  134.9 0.3 reshape.677
  135.3 0.3 copy.42
  135.6 1.8 %reshape_reshape.3 = f32[2,16,4,32,16]{4,3,2,1,0:T(8,128)} reshape(f32[2,16,4,8,64]{4,3,2,1,0:T(8,128)S(1)} %copy.42) | data formatting | bytes 524288 | tf_op jit(solution)/shard_map/reshape;reshape | solution.py:89
  137.4 5.1 %fusion.3 = f32[256,2,16,4,16,1]{0,4,1,5,3,2:T(8,128)S(1)} fusion(f32[256,1,2,32]{0,3,2,1:T(8,128)S(1)} %get-tuple-element.16, f32[256,1,2,32]{0,3,2,1:T(8,128)S(1)} %get-tuple-element.13, f32[2,16,4,32,16]{4,3,2,1,0:T(8,128)} %reshape_reshape.3), kind=kOutput, calls=%fused_computation.11 | convolution fusion | flops 402685952 | bytes 2490368 | tf_op jit(solution)/shard_map/pcxjl,ypqj->cxqly/dot_general | solution.py:91
  142.4 14.9 %bitcast_convert_fusion = bf16[16,4,256,128]{3,2,1,0:T(8,128)(2,1)} fusion(f32[256,2,16,4,16,1]{0,4,1,5,3,2:T(8,128)S(1)} %fusion.3, f32[1,16,128]{2,1,0:T(8,128)S(1)} %get-tuple-element.22, f32[1,16,128]{2,1,0:T(8,128)S(1)} %get-tuple-element.21), kind=kOutput, calls=%fused_computation | convolution fusion | flops 807407616 | bytes 6307840 | tf_op jit(solution)/shard_map/cxqly,qlz->cxyz/dot_general | solution.py:92
  (29 shorter events, 0.4 us)
Async XLA Ops:
  6.5 41.3 %copy-start = (f32[2,8,32,8,8,4]{2,5,4,3,1,0:T(4,128)S(1)}, f32[2,8,32,8,8,4]{2,5,4,3,1,0:T(4,128)}, u32[]{:S(2)}) copy-start(f32[2,8,32,8,8,4]{2,5,4,3,1,0:T(4,128)} %param.9) | copy-start | bytes 1572868
  17.9 11.3 %copy-start.5 = (f32[32,8]{0,1:T(8,128)S(1)}, f32[32,8]{0,1:T(8,128)}, u32[]{:S(2)}) copy-start(f32[32,8]{0,1:T(8,128)} %param.13) | copy-start | bytes 3076
  21.6 16.2 %all-to-all-start = ((f32[8,1,8192]{2,1,0:T(1,128)}), f32[8,1,8192]{2,1,0:T(1,128)S(1)}, u32[]{:S(2)}, u32[]{:S(2)}) async-start(f32[8,1,8192]{2,1,0:T(1,128)} %reshape.674), calls=%async_computation | async-start | bytes 524288 | tf_op jit(solution)/shard_map/all_to_all | solution.py:59
  28.9 42.3 %reduce-scatter.2.cloned.1.call-start = ((), (), s32[]{:S(2)}) async-start(), calls=%async_computation.3 | async-start | bytes 1310720 | tf_op jit(solution)/shard_map/reduce_scatter | solution.py:62
  42.3 2.6 %copy-start.1 = (f32[16,32]{1,0:T(8,128)S(1)}, f32[16,32]{1,0:T(8,128)}, u32[]{:S(2)}) copy-start(f32[16,32]{1,0:T(8,128)} %param.10) | copy-start | bytes 6148
  44.2 3.2 %copy-start.6 = (f32[16,4]{0,1:T(4,128)S(1)}, f32[16,4]{0,1:T(4,128)}, u32[]{:S(2)}) copy-start(f32[16,4]{0,1:T(4,128)} %param.14) | copy-start | bytes 772
  44.2 3.4 %copy-start.3 = (s32[32,16]{0,1:T(8,128)S(1)}, s32[32,16]{0,1:T(8,128)}, u32[]{:S(2)}) copy-start(s32[32,16]{0,1:T(8,128)} %param.15) | copy-start | bytes 6148
  47.2 68.5 %all-reduce.2.cloned.1.call-start = ((), (), s32[]{:S(2)}) async-start(), calls=%async_computation.4 | async-start | bytes 2097152 | tf_op jit(solution)/shard_map/psum | solution.py:81
  47.9 3.8 %copy-start.4 = (f32[32,8]{0,1:T(8,128)S(1)}, f32[32,8]{0,1:T(8,128)}, u32[]{:S(2)}) copy-start(f32[32,8]{0,1:T(8,128)} %param.12) | copy-start | bytes 3076
  77.5 38.2 %copy-start.2 = (f32[16,32]{1,0:T(8,128)S(1)}, f32[16,32]{1,0:T(8,128)}, u32[]{:S(2)}) copy-start(f32[16,32]{1,0:T(8,128)} %param.11) | copy-start | bytes 6148
  119.7 14.0 %all-to-all-start.1 = ((f32[8,1,8192]{2,1,0:T(1,128)}), f32[8,1,8192]{2,1,0:T(1,128)S(1)}, u32[]{:S(2)}, u32[]{:S(2)}) async-start(f32[8,1,8192]{2,1,0:T(1,128)} %reshape.676), calls=%async_computation.2 | async-start | bytes 524288 | tf_op jit(solution)/shard_map/all_to_all | solution.py:86
Sparse Core Ops, SparseCore 0:
  47.3 23.8 reduce-scatter.1
  79.3 36.2 all-reduce.1
